TPU v7x, 32 devices: a whole 2x2x4 slice. The times are simulated.
32 devices in a mesh: grid: 8 (over y, x, core), rows: 4 (over z).
Axes of the slice: x: 2, y: 2, z: 4, core: 2. Of those that a mesh axis runs over, the one named last changes fastest.
Arguments:
- density: bfloat16 [32, 128, 4096], P(None, 'rows', 'grid'), as said below
- basis_values: bfloat16 [16, 16, 128, 512], P('grid', None, 'rows'), may hold values from -0.59765625 to 0.59765625
- grid_points: float32 [16, 3, 512], P('grid'), may hold values from -4 to 4
- grid_weights: float32 [16, 512], P('grid'), may hold values from 0.05 to 1
- screened_blocks: int32 [16, 16], P('grid'), may hold values from 0 to 31, as said below
Outputs:
- exchange: float32 [32, 128, 4096], P(None, 'rows', 'grid')
Inputs may be any that keep to these rules, and one draw needn't show every extreme that they name: density is symmetric: density[a, i, b * 128 + j] equals density[b, j, a * 128 + i]. `screened_blocks`: each row holds 16 distinct block numbers.
All inputs are finite; a program needn't handle non-finite values.
Results may differ from a plain program's by a relative error of at most 0.00055.
The roundings to bfloat16 on the way count: a program that leaves them out, or rounds other values in their place, can miss the bound.
Values may be sent and summed in bfloat16 or wider, within the bound.
A program may use at most 128 MiB of HBM per device.

v0:
```python
import jax
import jax.numpy as jnp
from jax import lax
from jax.sharding import PartitionSpec as P


def body(density, basis_values, grid_points, grid_weights, screened_blocks):
    nblocks = density.shape[0]
    rows_mine = density.shape[1]
    block_size = rows_mine * lax.axis_size("rows")
    nbasis = nblocks * block_size
    nsig = basis_values.shape[1]
    npoints = basis_values.shape[3]
    stripe = lax.all_gather(density, "grid", axis=2, tiled=True)
    totals = jnp.zeros((nblocks, rows_mine, nblocks, block_size), jnp.float32)
    for batch_index in range(basis_values.shape[0]):
        blocks = screened_blocks[batch_index]
        row_pick = jnp.take(stripe, blocks, axis=0).reshape(nsig * rows_mine, nblocks, block_size)
        chosen = jnp.take(row_pick, blocks, axis=1)
        local_values = basis_values[batch_index]
        x_mine = local_values.reshape(nsig * rows_mine, npoints)
        fsum = jnp.einsum(
            "mtk,tkp->mp",
            chosen,
            lax.all_gather(local_values, "rows", axis=1, tiled=True),
            preferred_element_type=jnp.float32,
        )
        fmat = fsum.astype(jnp.bfloat16)
        intersection_part = lax.dot_general(
            x_mine, fmat, (((0,), (0,)), ((), ())), preferred_element_type=jnp.float32
        )
        intersection = lax.psum(intersection_part, "rows")
        places = grid_points[batch_index]
        weights = grid_weights[batch_index]
        diffs = places[:, :, None] - places[:, None, :]
        kern = 1.0 / jnp.sqrt(jnp.sum(diffs * diffs, axis=0) + 0.5)
        mixed = (weights[:, None] * kern * intersection).astype(jnp.bfloat16)
        potential = (
            jnp.dot(x_mine, mixed, preferred_element_type=jnp.float32) * weights[None, :]
        ).astype(jnp.bfloat16)
        potential = potential.reshape(nsig, rows_mine, npoints)
        block_k = jnp.einsum(
            "mp,tkp->mtk",
            x_mine,
            lax.all_gather(potential, "rows", axis=1, tiled=True),
            preferred_element_type=jnp.float32,
        )
        block_k = block_k.reshape(nsig, rows_mine, nsig, block_size)
        totals = totals.at[blocks[:, None], :, blocks[None, :], :].add(
            block_k.transpose(0, 2, 1, 3)
        )
    return lax.psum_scatter(
        totals.reshape(nblocks, rows_mine, nbasis), "grid", scatter_dimension=2, tiled=True
    )


def solution(mesh):
    placed = (
        P(None, "rows", "grid"),
        P("grid", None, "rows", None),
        P("grid", None, None),
        P("grid", None),
        P("grid", None),
    )
    return jax.shard_map(
        body, mesh=mesh, in_specs=placed, out_specs=P(None, "rows", "grid"), check_vma=False
    )
```

profile of v0, /device:TPU:0, one launch (start us, length us, event | category | flops | bytes accessed | tf_op | source)
XLA Modules:
  0.0 572.5 jit_solution(16403228100501752769)
XLA Ops:
  6.5 0.0 copy-start.4
  6.5 0.0 all-gather.8.cloned.1.call-start
  6.5 0.7 all-gather.8.cloned.1.call-update
  7.3 0.0 all-gather.16.cloned.1.call-start
  7.3 2.3 fusion.56
  9.6 0.0 all-gather.16.cloned.1.call-update
  9.6 0.0 all-gather.14.cloned.1.call-start
  9.7 0.7 all-gather.14.cloned.1.call-update
  10.4 0.0 all-reduce.3.cloned.1.call-start
  10.4 0.0 copy-done.4
  10.5 57.3 %all-gather.8.cloned.1.call-done = bf16[32,32,4096]{2,1,0:T(8,128)(2,1)} async-done(((bf16[32,32,512]{2,1,0:T(8,128)(2,1)}), bf16[32,32,4096]{2,1,0:T(8,128)(2,1)}) %all-gather.8.cloned.1.call-update) | async-done | bytes 8388624 | tf_op jit(solution)/shard_map/all_gather | solution.py:14
  67.8 6.2 %gather_fusion.2 = bf16[16,32,4096]{2,1,0:T(8,128)(2,1)} fusion(bf16[32,32,4096]{2,1,0:T(8,128)(2,1)} %all-gather.8.cloned.1.call-done, s32[1024]{0:T(1024)S(1)} %pad_clamp_fusion), kind=kCustom, calls=%fused_computation.2.clone | custom fusion | bytes 8388672 | tf_op jit(solution)/shard_map/jit(_take)/gather | solution.py:18
  74.0 2.7 broadcast_select_fusion
  76.7 1.3 copy.31
  78.0 3.6 copy.23
  81.6 3.1 gather_fusion.3
  84.8 6.2 %gather_fusion = bf16[16,32,4096]{2,1,0:T(8,128)(2,1)} fusion(bf16[32,32,4096]{2,1,0:T(8,128)(2,1)} %all-gather.8.cloned.1.call-done, s32[1024]{0:T(1024)S(1)} %pad_clamp_fusion.1), kind=kCustom, calls=%fused_computation.clone | custom fusion | bytes 8388672 | tf_op jit(solution)/shard_map/jit(_take)/gather | solution.py:18
  91.0 2.7 broadcast_select_fusion.1
  93.6 1.3 copy.30
  94.9 3.6 copy.19
  98.5 0.0 copy-start
  98.5 4.4 gather_fusion.1
  102.9 12.2 %all-gather.16.cloned.1.call-done = bf16[1,16,128,512]{3,2,1,0:T(8,128)(2,1)} async-done(((bf16[1,16,32,512]{3,2,1,0:T(8,128)(2,1)}), bf16[1,16,128,512]{3,2,1,0:T(8,128)(2,1)}) %all-gather.16.cloned.1.call-update) | async-done | bytes 2097168 | tf_op jit(solution)/shard_map/all_gather | solution.py:25
  115.1 0.0 copy-done
  115.1 0.0 copy-start.1
  115.1 4.3 convolution_bitcast_fusion.2
  119.4 41.8 %all-gather.14.cloned.1.call-done = bf16[1,16,128,512]{3,2,1,0:T(8,128)(2,1)} async-done(((bf16[1,16,32,512]{3,2,1,0:T(8,128)(2,1)}), bf16[1,16,128,512]{3,2,1,0:T(8,128)(2,1)}) %all-gather.14.cloned.1.call-update) | async-done | bytes 2097168 | tf_op jit(solution)/shard_map/all_gather | solution.py:25
  161.2 0.0 copy-done.1
  161.2 0.0 copy-start.2
  161.2 4.9 convolution_bitcast_fusion.3
  166.0 0.0 copy-start.3
  166.0 0.0 all-reduce.3.cloned.1.call-update
  166.1 0.0 all-gather.10.cloned.1.call-start
  166.1 0.0 copy-done.2
  166.2 0.4 multiply_reduce_fusion.1
  166.5 0.3 copy.18
  166.9 0.0 copy-done.3
  166.9 84.3 %all-reduce.3.cloned.1.call-done = (f32[512,512]{0,1:T(8,128)}, f32[512,512]{0,1:T(8,128)}) async-done(((f32[512,512]{0,1:T(8,128)}, f32[512,512]{0,1:T(8,128)}), (f32[512,512]{0,1:T(8,128)}, f32[512,512]{0,1:T(8,128)})) %all-reduce.3.cloned.1.call-update) | async-done | bytes 2097168 | tf_op jit(solution)/shard_map/psum | solution.py:32
  251.2 2.5 fusion.20
  253.7 0.0 all-gather.10.cloned.1.call-update
  253.7 0.0 all-gather.12.cloned.1.call-start
  253.8 0.4 multiply_reduce_fusion
  254.2 0.3 copy.22
  254.5 2.5 fusion.21
  257.0 0.0 all-gather.12.cloned.1.call-update
  257.0 0.2 reduce-scatter.2.cloned.1.call-start
  257.3 0.1 or_select_fusion
  257.4 0.1 reshape.132
  257.5 0.1 reshape.138
  257.6 41.0 %all-gather.10.cloned.1.call-done = bf16[16,128,512]{2,1,0:T(8,128)(2,1)} async-done(((bf16[16,32,512]{2,1,0:T(8,128)(2,1)}), bf16[16,128,512]{2,1,0:T(8,128)(2,1)}) %all-gather.10.cloned.1.call-update) | async-done | bytes 2097168 | tf_op jit(solution)/shard_map/all_gather | solution.py:45
  298.6 4.8 convolution_bitcast_fusion.1
  303.4 5.5 copy.20
  309.0 5.5 copy.21
  314.4 30.1 %all-gather.12.cloned.1.call-done = bf16[16,128,512]{2,1,0:T(8,128)(2,1)} async-done(((bf16[16,32,512]{2,1,0:T(8,128)(2,1)}), bf16[16,128,512]{2,1,0:T(8,128)(2,1)}) %all-gather.12.cloned.1.call-update) | async-done | bytes 2097168 | tf_op jit(solution)/shard_map/all_gather | solution.py:45
  344.5 4.8 convolution_bitcast_fusion
  349.3 5.5 copy.24
  354.8 5.5 copy.25
  360.3 7.9 %broadcast_in_dim.45 = f32[32,32,32,128]{3,1,2,0:T(8,128)} broadcast(f32[]{:T(128)} %constant.20.clone.1), dimensions={} | broadcast | bytes 16777220 | tf_op jit(solution)/shard_map/broadcast_in_dim | solution.py:15
  368.2 35.3 %scatter_fusion = f32[32,32,32,128]{3,1,2,0:T(8,128)} fusion(f32[32,32,32,128]{3,1,2,0:T(8,128)} %broadcast_in_dim.45, s32[256]{0:T(256)S(1)} %reshape.132, f32[256,32,128]{2,1,0:T(8,128)} %bitcast.123), kind=kCustom, calls=%fused_computation.4 | custom fusion | flops 1048576 | bytes 12584960 | tf_op jit(solution)/shard_map/scatter-add | solution.py:49
  403.5 35.3 %scatter_fusion.1 = f32[32,32,32,128]{3,1,2,0:T(8,128)} fusion(f32[32,32,32,128]{3,1,2,0:T(8,128)} %scatter_fusion, s32[256]{0:T(256)S(1)} %reshape.138, f32[256,32,128]{2,1,0:T(8,128)} %bitcast.124), kind=kCustom, calls=%fused_computation.5 | custom fusion | flops 1048576 | bytes 12584960 | tf_op jit(solution)/shard_map/scatter-add | solution.py:49
  438.9 11.7 %copy_bitcast_fusion = f32[32,32,4096]{2,1,0:T(8,128)} fusion(f32[32,32,32,128]{3,1,2,0:T(8,128)} %scatter_fusion.1), kind=kLoop, calls=%fused_computation.6 | loop fusion | bytes 33554432 | tf_op jit(solution)/shard_map/reshape | solution.py:53
  450.6 0.0 reduce-scatter.2.cloned.1.call-update
  450.6 115.0 %reduce-scatter.2.cloned.1.call-done = f32[32,32,512]{2,1,0:T(8,128)} async-done(((f32[32,32,4096]{2,1,0:T(8,128)}), f32[32,32,512]{2,1,0:T(8,128)}) %reduce-scatter.2.cloned.1.call-update) | async-done | bytes 2097168 | tf_op jit(solution)/shard_map/reduce_scatter | solution.py:52
  (11 shorter events, 0.1 us)
Async XLA Ops:
  6.5 3.9 copy-start.4
  6.5 61.3 %all-gather.8.cloned.1.call-start = ((), (), s32[]{:S(2)}) async-start(), calls=%async_computation.1 | async-start | bytes 9437184 | tf_op jit(solution)/shard_map/all_gather | solution.py:14
  7.3 107.8 %all-gather.16.cloned.1.call-start = ((), (), s32[]{:S(2)}) async-start(), calls=%async_computation.6 | async-start | bytes 2621440 | tf_op jit(solution)/shard_map/all_gather | solution.py:25
  9.6 151.5 %all-gather.14.cloned.1.call-start = ((), (), s32[]{:S(2)}) async-start(), calls=%async_computation.5 | async-start | bytes 2621440 | tf_op jit(solution)/shard_map/all_gather | solution.py:25
  10.4 240.8 %all-reduce.3.cloned.1.call-start = ((), (), s32[]{:S(2)}) async-start(), calls=%async_computation.7 | async-start | bytes 4194304 | tf_op jit(solution)/shard_map/psum | solution.py:32
  98.5 16.6 %copy-start = (bf16[1,16,32,512]{3,2,1,0:T(8,128)(2,1)S(1)}, bf16[1,16,32,512]{3,2,1,0:T(8,128)(2,1)}, u32[]{:S(2)}) copy-start(bf16[1,16,32,512]{3,2,1,0:T(8,128)(2,1)} %get-tuple-element.13) | copy-start | bytes 1572868
  115.1 46.1 %copy-start.1 = (bf16[1,16,32,512]{3,2,1,0:T(8,128)(2,1)S(1)}, bf16[1,16,32,512]{3,2,1,0:T(8,128)(2,1)}, u32[]{:S(2)}) copy-start(bf16[1,16,32,512]{3,2,1,0:T(8,128)(2,1)} %get-tuple-element.14) | copy-start | bytes 1572868
  161.2 5.0 copy-start.2
  166.0 0.8 copy-start.3
  166.1 132.5 %all-gather.10.cloned.1.call-start = ((), (), s32[]{:S(2)}) async-start(), calls=%async_computation.2 | async-start | bytes 2621440 | tf_op jit(solution)/shard_map/all_gather | solution.py:45
  253.7 90.8 %all-gather.12.cloned.1.call-start = ((), (), s32[]{:S(2)}) async-start(), calls=%async_computation.3 | async-start | bytes 2621440 | tf_op jit(solution)/shard_map/all_gather | solution.py:45
  257.0 308.6 %reduce-scatter.2.cloned.1.call-start = ((), (), s32[]{:S(2)}) async-start(), calls=%async_computation.4 | async-start | bytes 18874368 | tf_op jit(solution)/shard_map/reduce_scatter | solution.py:52
Sparse Core Ops, SparseCore 0:
  9.2 58.5 all-gather.7
  69.4 45.6 all-gather.15
  116.7 44.4 all-gather.13
  166.2 84.9 all-reduce.2
  253.9 44.6 all-gather.9
  300.0 44.4 all-gather.11
  450.7 114.8 reduce-scatter.1
where the time goes:
time: 574 us; the launch traced here: 572 us
  waiting for transfers between devices  383 us (67%)
  other arithmetic  76.9 us (13%)
  local copies, waits for them, and re-layouts  74.4 us (13%)
  matrix products  23.9 us (4%)
  between operations  13.7 us (2%)
    reduce_scatter x1, waiting for transfers between devices, body(): lax.psum_scatter(totals.reshape(nblocks, rows_mine, nbasis), 'grid', scat...  115 us
    psum x1, waiting for transfers between devices, body(): intersection = lax.psum(intersection_part, 'rows')  84.3 us
    all_gather x2, waiting for transfers between devices, body(): lax.all_gather(potential, 'rows', axis=1, tiled=True)  71.1 us
    scatter-add x2, other arithmetic, body(): totals.at[blocks[:, None], :, blocks[None, :], :]  70.6 us
    all_gather x1, waiting for transfers between devices, body(): stripe = lax.all_gather(density, 'grid', axis=2, tiled=True)  57.3 us
    all_gather x2, waiting for transfers between devices, body(): lax.all_gather(local_values, 'rows', axis=1, tiled=True)  53.9 us
    gather x2, local copies, waits for them, and re-layouts, body(): jnp.take(stripe, blocks, axis=0)  12.4 us
    reshape x1, local copies, waits for them, and re-layouts, body(): totals.reshape(nblocks, rows_mine, nbasis)  11.7 us
  transfers between devices with their start and end apart: 7, of which 7 were waited for; matrix products, arithmetic and copies ran while one was open for 11% of the time, Pallas kernels for 0%

commit v1 on v0

--- a/solution.py
+++ b/solution.py
@@ -29,7 +29,7 @@
         intersection_part = lax.dot_general(
             x_mine, fmat, (((0,), (0,)), ((), ())), preferred_element_type=jnp.float32
         )
-        intersection = lax.psum(intersection_part, "rows")
+        intersection = jnp.sum(lax.all_gather(intersection_part, "rows"), axis=0)
         places = grid_points[batch_index]
         weights = grid_weights[batch_index]
         diffs = places[:, :, None] - places[:, None, :]

time: 574 us -> 644 us (1.12)
  waiting for transfers between devices: 383 us -> 435 us
  local copies, waits for them, and re-layouts: 74.4 us -> 85.3 us
  other arithmetic: 76.9 us -> 87.1 us
    all_gather x0 -> x2, waiting for transfers between devices: none -> 143 us  [body(): intersection = jnp.sum(lax.all_gather(intersection_part, 'rows'), axis=0)]
    psum x1 -> x0, waiting for transfers between devices: 84.3 us -> none  [body(): intersection = lax.psum(intersection_part, 'rows')]
    all_gather x0 -> x2, local copies, waits for them, and re-layouts: none -> 12.1 us  [body(): intersection = jnp.sum(lax.all_gather(intersection_part, 'rows'), axis=0)]
    reduce_sum x0 -> x2, other arithmetic: none -> 10.2 us  [body(): intersection = jnp.sum(lax.all_gather(intersection_part, 'rows'), axis=0)]
    all_gather x2, waiting for transfers between devices: 71.1 us -> 62.9 us  [body(): lax.all_gather(potential, 'rows', axis=1, tiled=True)]
  transfers between devices with their start and end apart: 7 -> 8, of which waited for: 7 -> 8; matrix products, arithmetic and copies ran while one was open for 11% -> 14% of each run, Pallas kernels for 0% -> 0%
where the time goes in v1:
time: 644 us; the launch traced here: 642 us
  waiting for transfers between devices  435 us (68%)
  other arithmetic  87.1 us (14%)
  local copies, waits for them, and re-layouts  85.3 us (13%)
  matrix products  20.8 us (3%)
  between operations  13.7 us (2%)
    all_gather x2, waiting for transfers between devices, body(): intersection = jnp.sum(lax.all_gather(intersection_part, 'rows'), axis=0)  143 us
    reduce_scatter x1, waiting for transfers between devices, body(): lax.psum_scatter(totals.reshape(nblocks, rows_mine, nbasis), 'grid', scat...  115 us
    scatter-add x2, other arithmetic, body(): totals.at[blocks[:, None], :, blocks[None, :], :]  70.7 us
    all_gather x2, waiting for transfers between devices, body(): lax.all_gather(potential, 'rows', axis=1, tiled=True)  62.9 us
    all_gather x1, waiting for transfers between devices, body(): stripe = lax.all_gather(density, 'grid', axis=2, tiled=True)  57.4 us
    all_gather x2, waiting for transfers between devices, body(): lax.all_gather(local_values, 'rows', axis=1, tiled=True)  55 us
  transfers between devices with their start and end apart: 8, of which 8 were waited for; matrix products, arithmetic and copies ran while one was open for 14% of the time, Pallas kernels for 0%

profile of v1, /device:TPU:0, one launch (start us, length us, event | category | flops | bytes accessed | tf_op | source)
XLA Modules:
  0.0 642.5 jit_solution(6307232178698835145)
XLA Ops:
  6.5 0.0 all-gather.12.cloned.1.call-start
  6.5 0.7 all-gather.12.cloned.1.call-update
  7.3 0.0 all-gather.18.cloned.1.call-start
  7.3 2.3 fusion.56
  9.6 0.0 all-gather.18.cloned.1.call-update
  9.6 0.0 all-gather.22.cloned.1.call-start
  9.7 0.7 all-gather.22.cloned.1.call-update
  10.3 0.0 all-gather.20.cloned.1.call-start
  10.4 0.0 copy-done.4
  10.4 57.4 %all-gather.12.cloned.1.call-done = bf16[32,32,4096]{2,1,0:T(8,128)(2,1)} async-done(((bf16[32,32,512]{2,1,0:T(8,128)(2,1)}), bf16[32,32,4096]{2,1,0:T(8,128)(2,1)}) %all-gather.12.cloned.1.call-update) | async-done | bytes 8388624 | tf_op jit(solution)/shard_map/all_gather | solution.py:14
  67.8 6.2 gather_fusion
  74.0 2.7 broadcast_select_fusion.1
  76.7 1.3 copy.30
  78.0 3.6 copy.19
  81.6 3.2 gather_fusion.1
  84.8 30.3 %all-gather.18.cloned.1.call-done = bf16[1,16,128,512]{3,2,1,0:T(8,128)(2,1)} async-done(((bf16[1,16,32,512]{3,2,1,0:T(8,128)(2,1)}), bf16[1,16,128,512]{3,2,1,0:T(8,128)(2,1)}) %all-gather.18.cloned.1.call-update) | async-done | bytes 2097168 | tf_op jit(solution)/shard_map/all_gather | solution.py:25
  115.1 0.0 copy-done.1
  115.1 4.2 convolution_bitcast_fusion.3
  119.3 0.0 all-gather.20.cloned.1.call-update
  119.4 0.0 all-gather.24.cloned.1.call-start
  119.4 6.3 gather_fusion.2
  125.7 2.6 broadcast_select_fusion
  128.4 1.3 copy.31
  129.6 3.6 copy.23
  133.2 3.2 gather_fusion.3
  136.4 24.7 %all-gather.22.cloned.1.call-done = bf16[1,16,128,512]{3,2,1,0:T(8,128)(2,1)} async-done(((bf16[1,16,32,512]{3,2,1,0:T(8,128)(2,1)}), bf16[1,16,128,512]{3,2,1,0:T(8,128)(2,1)}) %all-gather.22.cloned.1.call-update) | async-done | bytes 2097168 | tf_op jit(solution)/shard_map/all_gather | solution.py:25
  161.2 0.0 copy-done
  161.2 4.3 convolution_bitcast_fusion.2
  165.5 0.0 all-gather.24.cloned.1.call-update
  165.5 0.2 all-gather.14.cloned.1.call-start
  165.8 0.0 copy-done.2
  165.8 0.4 multiply_reduce_fusion.1
  166.2 0.3 copy.18
  166.5 75.6 %all-gather.20.cloned.1.call-done = f32[2048,512]{0,1:T(8,128)} async-done(((f32[512,512]{0,1:T(8,128)}), f32[2048,512]{0,1:T(8,128)}) %all-gather.20.cloned.1.call-update) | async-done | bytes 4194320 | tf_op jit(solution)/shard_map/all_gather | solution.py:32
  242.2 6.1 reshape.145
  248.2 5.2 reduce_sum.37
  253.4 1.3 fusion.20
  254.7 0.0 all-gather.14.cloned.1.call-update
  254.7 0.0 all-gather.16.cloned.1.call-start
  254.8 0.4 multiply_reduce_fusion
  255.2 0.3 copy.22
  255.5 67.3 %all-gather.24.cloned.1.call-done = f32[2048,512]{0,1:T(8,128)} async-done(((f32[512,512]{0,1:T(8,128)}), f32[2048,512]{0,1:T(8,128)}) %all-gather.24.cloned.1.call-update) | async-done | bytes 4194320 | tf_op jit(solution)/shard_map/all_gather | solution.py:32
  322.8 6.1 reshape.147
  328.9 5.0 reduce_sum.39
  333.9 1.3 fusion.21
  335.2 0.0 all-gather.16.cloned.1.call-update
  335.2 0.3 reduce-scatter.2.cloned.1.call-start
  335.6 0.1 or_select_fusion
  335.7 0.1 reshape.138
  335.7 0.1 reshape.132
  335.8 32.6 %all-gather.14.cloned.1.call-done = bf16[16,128,512]{2,1,0:T(8,128)(2,1)} async-done(((bf16[16,32,512]{2,1,0:T(8,128)(2,1)}), bf16[16,128,512]{2,1,0:T(8,128)(2,1)}) %all-gather.14.cloned.1.call-update) | async-done | bytes 2097168 | tf_op jit(solution)/shard_map/all_gather | solution.py:45
  368.4 4.8 convolution_bitcast_fusion.1
  373.3 5.5 copy.20
  378.8 5.4 copy.21
  384.2 30.3 %all-gather.16.cloned.1.call-done = bf16[16,128,512]{2,1,0:T(8,128)(2,1)} async-done(((bf16[16,32,512]{2,1,0:T(8,128)(2,1)}), bf16[16,128,512]{2,1,0:T(8,128)(2,1)}) %all-gather.16.cloned.1.call-update) | async-done | bytes 2097168 | tf_op jit(solution)/shard_map/all_gather | solution.py:45
  414.5 4.8 convolution_bitcast_fusion
  419.3 5.5 copy.24
  424.8 5.5 copy.25
  430.3 7.9 %broadcast_in_dim.45 = f32[32,32,32,128]{3,1,2,0:T(8,128)} broadcast(f32[]{:T(128)} %constant.20.clone.1), dimensions={} | broadcast | bytes 16777220 | tf_op jit(solution)/shard_map/broadcast_in_dim | solution.py:15
  438.2 35.3 %scatter_fusion = f32[32,32,32,128]{3,1,2,0:T(8,128)} fusion(f32[32,32,32,128]{3,1,2,0:T(8,128)} %broadcast_in_dim.45, s32[256]{0:T(256)S(1)} %reshape.132, f32[256,32,128]{2,1,0:T(8,128)} %bitcast.127), kind=kCustom, calls=%fused_computation.4 | custom fusion | flops 1048576 | bytes 12584960 | tf_op jit(solution)/shard_map/scatter-add | solution.py:49
  473.5 35.4 %scatter_fusion.1 = f32[32,32,32,128]{3,1,2,0:T(8,128)} fusion(f32[32,32,32,128]{3,1,2,0:T(8,128)} %scatter_fusion, s32[256]{0:T(256)S(1)} %reshape.138, f32[256,32,128]{2,1,0:T(8,128)} %bitcast.128), kind=kCustom, calls=%fused_computation.5 | custom fusion | flops 1048576 | bytes 12584960 | tf_op jit(solution)/shard_map/scatter-add | solution.py:49
  508.9 11.7 %copy_bitcast_fusion = f32[32,32,4096]{2,1,0:T(8,128)} fusion(f32[32,32,32,128]{3,1,2,0:T(8,128)} %scatter_fusion.1), kind=kLoop, calls=%fused_computation.6 | loop fusion | bytes 33554432 | tf_op jit(solution)/shard_map/reshape | solution.py:53
  520.6 0.0 reduce-scatter.2.cloned.1.call-update
  520.6 115.1 %reduce-scatter.2.cloned.1.call-done = f32[32,32,512]{2,1,0:T(8,128)} async-done(((f32[32,32,4096]{2,1,0:T(8,128)}), f32[32,32,512]{2,1,0:T(8,128)}) %reduce-scatter.2.cloned.1.call-update) | async-done | bytes 2097168 | tf_op jit(solution)/shard_map/reduce_scatter | solution.py:52
  (17 shorter events, 0.1 us)
Async XLA Ops:
  6.5 3.9 copy-start.4
  6.5 61.3 %all-gather.12.cloned.1.call-start = ((), (), s32[]{:S(2)}) async-start(), calls=%async_computation.1 | async-start | bytes 9437184 | tf_op jit(solution)/shard_map/all_gather | solution.py:14
  7.3 107.8 %all-gather.18.cloned.1.call-start = ((), (), s32[]{:S(2)}) async-start(), calls=%async_computation.5 | async-start | bytes 2621440 | tf_op jit(solution)/shard_map/all_gather | solution.py:25
  9.6 151.6 %all-gather.22.cloned.1.call-start = ((), (), s32[]{:S(2)}) async-start(), calls=%async_computation.7 | async-start | bytes 2621440 | tf_op jit(solution)/shard_map/all_gather | solution.py:25
  10.3 231.8 %all-gather.20.cloned.1.call-start = ((), (), s32[]{:S(2)}) async-start(), calls=%async_computation.6 | async-start | bytes 5242880 | tf_op jit(solution)/shard_map/all_gather | solution.py:32
  81.6 33.5 %copy-start.1 = (bf16[1,16,32,512]{3,2,1,0:T(8,128)(2,1)S(1)}, bf16[1,16,32,512]{3,2,1,0:T(8,128)(2,1)}, u32[]{:S(2)}) copy-start(bf16[1,16,32,512]{3,2,1,0:T(8,128)(2,1)} %get-tuple-element.12) | copy-start | bytes 1572868
  119.4 203.5 %all-gather.24.cloned.1.call-start = ((), (), s32[]{:S(2)}) async-start(), calls=%async_computation.8 | async-start | bytes 5242880 | tf_op jit(solution)/shard_map/all_gather | solution.py:32
  133.2 27.9 %copy-start = (bf16[1,16,32,512]{3,2,1,0:T(8,128)(2,1)S(1)}, bf16[1,16,32,512]{3,2,1,0:T(8,128)(2,1)}, u32[]{:S(2)}) copy-start(bf16[1,16,32,512]{3,2,1,0:T(8,128)(2,1)} %get-tuple-element.11) | copy-start | bytes 1572868
  161.2 4.6 copy-start.2
  165.5 1.0 copy-start.3
  165.5 202.9 %all-gather.14.cloned.1.call-start = ((), (), s32[]{:S(2)}) async-start(), calls=%async_computation.2 | async-start | bytes 2621440 | tf_op jit(solution)/shard_map/all_gather | solution.py:45
  254.7 159.8 %all-gather.16.cloned.1.call-start = ((), (), s32[]{:S(2)}) async-start(), calls=%async_computation.3 | async-start | bytes 2621440 | tf_op jit(solution)/shard_map/all_gather | solution.py:45
  335.2 300.4 %reduce-scatter.2.cloned.1.call-start = ((), (), s32[]{:S(2)}) async-start(), calls=%async_computation.4 | async-start | bytes 18874368 | tf_op jit(solution)/shard_map/reduce_scatter | solution.py:52
Sparse Core Ops, SparseCore 0:
  9.2 58.5 all-gather.11
  69.4 45.6 all-gather.17
  116.7 44.4 all-gather.21
  162.6 79.5 all-gather.19
  243.6 79.2 all-gather.23
  324.3 44.1 all-gather.13
  370.0 44.4 all-gather.15
  520.7 114.9 reduce-scatter.1
